TPU v7x, 32 devices: a whole 2x2x4 slice. The times are simulated.
32 devices in a mesh: dp: 8 (over z, x), tensor: 4 (over y, core).
Axes of the slice: x: 2, y: 2, z: 4, core: 2. Of those that a mesh axis runs over, the one named last changes fastest.
Arguments:
- hidden_in: bfloat16 [4096, 2048], P('dp'), may hold values from -40 to 40
- seq_lens: int32 [8, 8], P('dp'), may hold values from 0 to 512, as said below
- norm1_gain: float32 [2048], replicated, may hold values from 0.5 to 1.5
- query_weight: bfloat16 [2048, 4096], P(None, 'tensor'), may hold values from -0.125 to 0.125
- key_weight: bfloat16 [2048, 512], P(None, 'tensor'), may hold values from -0.125 to 0.125
- value_weight: bfloat16 [2048, 512], P(None, 'tensor'), may hold values from -0.125 to 0.125
- query_gain: float32 [128], replicated, may hold values from 0.5 to 1.5
- key_gain: float32 [128], replicated, may hold values from 0.5 to 1.5
- out_weight: bfloat16 [4096, 2048], P('tensor'), may hold values from -0.75 to 0.75
- norm2_gain: float32 [2048], replicated, may hold values from 0.5 to 1.5
- w_gate_up: bfloat16 [16, 2048, 2, 768], P('dp', None, None, 'tensor'), may hold values from -0.125 to 0.125
- w_down: bfloat16 [16, 768, 2048], P('dp', 'tensor'), may hold values from -0.875 to 0.875
- routes: int32 [4096, 8], P('dp'), may hold values from 0 to 15, all different within a row; in each aligned block of 512 rows (0 to 511, 512 to 1023, ...) at most 384 rows name the same one
- route_weights: float32 [4096, 8], P('dp'), may hold values from 0.05 to 0.25
- out_grad: bfloat16 [4096, 2048], P('dp'), may hold values from -6 to 6
Outputs:
- hidden_out: bfloat16 [4096, 2048], P('dp')
- hidden_grad: bfloat16 [4096, 2048], P('dp')
- grad_norm1_gain: float32 [2048], replicated
- grad_query_weight: float32 [2048, 4096], P(None, 'tensor')
- grad_key_weight: float32 [2048, 512], P(None, 'tensor')
- grad_value_weight: float32 [2048, 512], P(None, 'tensor')
- grad_query_gain: float32 [128], replicated
- grad_key_gain: float32 [128], replicated
- grad_out_weight: float32 [4096, 2048], P('tensor')
- grad_norm2_gain: float32 [2048], replicated
- grad_w_gate_up: float32 [16, 2048, 2, 768], P('dp', None, None, 'tensor')
- grad_w_down: float32 [16, 768, 2048], P('dp', 'tensor')
Inputs may be any that keep to these rules, and one draw needn't show every extreme that they name: `seq_lens`: each row sums to 512; zeros are empty slots; some row holds a single sequence of 512. `routes`: A row names 8 different experts. In the rows of one index of dp no expert is named by more than 384 rows, a bound that some block reaches.
All inputs are finite; a program needn't handle non-finite values.
Results may differ from a plain program's by a relative error of at most 0.028.
Values may be sent and summed in bfloat16 or wider, within the bound.
A program may use at most 384 MiB of HBM per device.

v0:
```python
import math
import jax
import jax.numpy as jnp
from jax import lax
from jax.sharding import PartitionSpec as P

EPSILON = 1e-06
ROPE_BASE = 1000000.0


def rms_parts(values):
    inverse = lax.rsqrt(jnp.mean(values * values, axis=-1, keepdims=True) + EPSILON)
    return (values * inverse, inverse)


def rms_back(grad_hat, normal_hat, inverse):
    return inverse * (
        grad_hat - normal_hat * jnp.mean(grad_hat * normal_hat, axis=-1, keepdims=True)
    )


def rotary_tables(positions, head_dim):
    halves = jnp.arange(head_dim // 2, dtype=jnp.float32)
    inverse = jnp.exp(halves * (-2.0 * math.log(ROPE_BASE) / head_dim))
    angles = positions.astype(jnp.float32)[:, None] * inverse[None, :]
    return (jnp.cos(angles), jnp.sin(angles))


def rotate(values, cosine_table, sine_table):
    middle_index = values.shape[-1] // 2
    first_half = values[..., :middle_index]
    second = values[..., middle_index:]
    return jnp.concatenate(
        [
            first_half * cosine_table - second * sine_table,
            second * cosine_table + first_half * sine_table,
        ],
        axis=-1,
    )


def rotate_back(gradient, cosine_table, sine_table):
    middle_index = gradient.shape[-1] // 2
    first_half = gradient[..., :middle_index]
    second = gradient[..., middle_index:]
    return jnp.concatenate(
        [
            first_half * cosine_table + second * sine_table,
            second * cosine_table - first_half * sine_table,
        ],
        axis=-1,
    )


def sequence_layout(lengths, token_count):
    endings = jnp.cumsum(lengths)
    places = jnp.arange(token_count, dtype=jnp.int32)
    starts = jnp.sum(jnp.where(endings[None, :] <= places[:, None], lengths[None, :], 0), axis=1)
    return (places, starts)


def local(
    hidden_in,
    seq_lens,
    norm1_gain,
    query_weight,
    key_weight,
    value_weight,
    query_gain,
    key_gain,
    out_weight,
    norm2_gain,
    w_gate_up,
    w_down,
    routes,
    route_weights,
    out_grad,
):
    bf = jnp.bfloat16
    f32 = jnp.float32
    tokens, model_width = hidden_in.shape
    local_experts = w_gate_up.shape[0]
    hidden_part = w_gate_up.shape[3]
    head_dim = query_gain.shape[0]
    local_heads = query_weight.shape[1] // head_dim
    data_size = lax.axis_size("dp")
    tensor_size = lax.axis_size("tensor")
    quarter = tokens // tensor_size
    experts = local_experts * data_size
    score_scale = head_dim ** (-0.5)
    row0 = lax.axis_index("tensor") * quarter

    def mine(array):
        return lax.dynamic_slice_in_dim(array, row0, quarter, 0)

    expert_ids = jnp.arange(experts, dtype=jnp.int32)
    dense = jnp.sum(
        jnp.where(
            mine(routes)[:, :, None] == expert_ids[None, None, :],
            mine(route_weights)[:, :, None],
            0.0,
        ),
        axis=1,
    )
    dense_high = dense.astype(bf)
    dense_low = (dense - dense_high.astype(f32)).astype(bf)
    packed = jnp.concatenate([mine(out_grad), dense_high, dense_low], axis=1)
    gathered = lax.all_gather(packed, "dp", tiled=True)
    grads_all = gathered[:, :model_width]
    dense_all = gathered[:, model_width : model_width + experts].astype(f32) + gathered[
        :, model_width + experts :
    ].astype(f32)
    weight_all = lax.dynamic_slice_in_dim(
        dense_all, lax.axis_index("dp") * local_experts, local_experts, 1
    )
    rows = data_size * quarter
    units = local_experts * hidden_part
    own_weights = jnp.concatenate(
        [
            jnp.transpose(w_gate_up, (2, 0, 3, 1)).reshape(2, units, model_width),
            w_down.reshape(1, units, model_width),
        ],
        axis=0,
    )
    all_weights = lax.all_gather(own_weights, "tensor")
    weight_cols = jnp.broadcast_to(
        weight_all[:, None, :, None], (rows, tensor_size, local_experts, hidden_part)
    ).reshape(rows, tensor_size, units)
    hidden = hidden_in.astype(f32)
    hat_one, inv_one = rms_parts(hidden)
    normed = (hat_one * norm1_gain).astype(bf)
    query_proj = jnp.dot(normed, query_weight, preferred_element_type=f32).reshape(
        tokens, local_heads, head_dim
    )
    key_proj = jnp.dot(normed, key_weight, preferred_element_type=f32)
    value_low = jnp.dot(normed, value_weight, preferred_element_type=f32).astype(bf)
    places, starts = sequence_layout(seq_lens[0], tokens)
    cosine_table, sine_table = rotary_tables(places - starts, head_dim)
    query_hat, query_inv = rms_parts(query_proj)
    query_low = rotate(
        query_hat * query_gain, cosine_table[:, None, :], sine_table[:, None, :]
    ).astype(bf)
    key_hat, key_inv = rms_parts(key_proj)
    key_low = rotate(key_hat * key_gain, cosine_table, sine_table).astype(bf)
    visible = (places[None, :] <= places[:, None]) & (places[None, :] >= starts[:, None])
    scores = jnp.einsum("thd,sd->hts", query_low, key_low, preferred_element_type=f32) * score_scale
    exponent = jnp.where(visible[None], jnp.exp(scores), 0.0)
    totals = jnp.sum(exponent, axis=-1, keepdims=True)
    log_totals = jnp.log(totals)
    soft_low = (exponent / totals).astype(bf)
    mixed_low = (
        jnp.einsum("hts,sd->thd", soft_low, value_low, preferred_element_type=f32)
        .reshape(tokens, local_heads * head_dim)
        .astype(bf)
    )
    attention = lax.psum_scatter(
        jnp.dot(mixed_low, out_weight, preferred_element_type=f32).astype(bf), "tensor", tiled=True
    ).astype(f32)
    hidden_q = mine(hidden_in).astype(f32)
    hat_one_q, inv_one_q = rms_parts(hidden_q)
    middle = hidden_q + attention
    hat_two, inv_two = rms_parts(middle)
    normed_two = (hat_two * norm2_gain).astype(bf)
    inputs = lax.all_gather(normed_two, "dp", tiled=True)

    def project(left, which):
        return jnp.einsum("td,rud->tru", left, all_weights[:, which], preferred_element_type=f32)

    gate_act = project(inputs, 0)
    upward = project(inputs, 1)
    sigmoid_gate = jax.nn.sigmoid(gate_act)
    active = gate_act * sigmoid_gate * upward
    weighted_low = (weight_cols * active).astype(bf)
    mixture_part = jnp.einsum(
        "tru,rud->td", weighted_low, all_weights[:, 2], preferred_element_type=f32
    ).astype(bf)
    mixture = lax.psum_scatter(mixture_part, "dp", tiled=True).astype(f32)
    hidden_out = (middle + mixture).astype(bf)
    grad_active = weight_cols * project(grads_all, 2)
    grad_gate = (
        grad_active * upward * sigmoid_gate * (1.0 + gate_act * (1.0 - sigmoid_gate))
    ).astype(bf)
    grad_up = (grad_active * gate_act * sigmoid_gate).astype(bf)
    grad_normed_part = jnp.einsum(
        "tru,rud->td", grad_gate, all_weights[:, 0], preferred_element_type=f32
    ) + jnp.einsum("tru,rud->td", grad_up, all_weights[:, 1], preferred_element_type=f32)
    grad_normed_two = lax.psum_scatter(grad_normed_part.astype(bf), "dp", tiled=True).astype(f32)
    weight_grads = jnp.stack(
        [
            jnp.einsum("tru,td->rud", grad_gate, inputs, preferred_element_type=f32).astype(bf),
            jnp.einsum("tru,td->rud", grad_up, inputs, preferred_element_type=f32).astype(bf),
            jnp.einsum("tru,td->rud", weighted_low, grads_all, preferred_element_type=f32).astype(
                bf
            ),
        ],
        axis=1,
    )
    own_grads = (
        lax.psum_scatter(weight_grads.reshape(-1, model_width), "tensor", tiled=True)
        .astype(f32)
        .reshape(3, units, model_width)
    )
    grad_w_gate_up = jnp.transpose(
        own_grads[:2].reshape(2, local_experts, hidden_part, model_width), (1, 3, 0, 2)
    )
    grad_w_down = own_grads[2].reshape(local_experts, hidden_part, model_width)
    grad_out = mine(out_grad).astype(f32)
    grad_gain_two = jnp.sum(grad_normed_two * hat_two, axis=0)
    grad_middle = grad_out + rms_back(grad_normed_two * norm2_gain, hat_two, inv_two)
    grad_mid_low = lax.all_gather(grad_middle.astype(bf), "tensor", tiled=True)
    grad_out_weight = jnp.einsum("ti,td->id", mixed_low, grad_mid_low, preferred_element_type=f32)
    grad_mixed = (
        jnp.einsum("td,id->ti", grad_mid_low, out_weight, preferred_element_type=f32)
        .astype(bf)
        .reshape(tokens, local_heads, head_dim)
    )
    scores_again = (
        jnp.einsum("thd,sd->hts", query_low, key_low, preferred_element_type=f32) * score_scale
    )
    soft_again = jnp.where(visible[None], jnp.exp(scores_again - log_totals), 0.0)
    grad_soft = jnp.einsum("thd,sd->hts", grad_mixed, value_low, preferred_element_type=f32)
    grad_scores = (
        soft_again * (grad_soft - jnp.sum(soft_again * grad_soft, axis=-1, keepdims=True))
    ).astype(bf)
    grad_values = jnp.einsum(
        "hts,thd->sd", soft_again.astype(bf), grad_mixed, preferred_element_type=f32
    ).astype(bf)
    grad_query_rot = score_scale * jnp.einsum(
        "hts,sd->thd", grad_scores, key_low, preferred_element_type=f32
    )
    grad_key_rot = score_scale * jnp.einsum(
        "hts,thd->sd", grad_scores, query_low, preferred_element_type=f32
    )
    grad_query_norm = rotate_back(grad_query_rot, cosine_table[:, None, :], sine_table[:, None, :])
    grad_query_gain = jnp.sum(grad_query_norm * query_hat, axis=(0, 1))
    grad_query_low = (
        rms_back(grad_query_norm * query_gain, query_hat, query_inv)
        .reshape(tokens, local_heads * head_dim)
        .astype(bf)
    )
    grad_key_norm = rotate_back(grad_key_rot, cosine_table, sine_table)
    grad_key_gain = jnp.sum(grad_key_norm * key_hat, axis=0)
    grad_key_low = rms_back(grad_key_norm * key_gain, key_hat, key_inv).astype(bf)
    grad_query_weight = jnp.einsum("ti,tj->ij", normed, grad_query_low, preferred_element_type=f32)
    grad_key_weight = jnp.einsum("ti,tj->ij", normed, grad_key_low, preferred_element_type=f32)
    grad_value_weight = jnp.einsum("ti,tj->ij", normed, grad_values, preferred_element_type=f32)
    grad_normed_one = jnp.einsum(
        "tj,ij->ti", grad_query_low, query_weight, preferred_element_type=f32
    )
    grad_normed_one = grad_normed_one + jnp.einsum(
        "tj,ij->ti", grad_key_low, key_weight, preferred_element_type=f32
    )
    grad_normed_one = grad_normed_one + jnp.einsum(
        "tj,ij->ti", grad_values, value_weight, preferred_element_type=f32
    )
    grad_normed_one = lax.psum_scatter(grad_normed_one.astype(bf), "tensor", tiled=True).astype(f32)
    grad_gain_one = jnp.sum(grad_normed_one * hat_one_q, axis=0)
    grad_hidden = grad_middle + rms_back(grad_normed_one * norm1_gain, hat_one_q, inv_one_q)
    both = lax.all_gather(
        jnp.stack([hidden_out, grad_hidden.astype(bf)], axis=0), "tensor", axis=1, tiled=True
    )
    grad_out_sum = lax.psum(grad_out_weight.astype(bf), "dp").astype(f32)
    summed = (
        lax.psum(grad_query_weight.astype(bf), "dp").astype(f32),
        lax.psum(grad_key_weight.astype(bf), "dp").astype(f32),
        lax.psum(grad_value_weight.astype(bf), "dp").astype(f32),
    )
    gains = lax.psum(
        jnp.concatenate([grad_gain_one, grad_gain_two, grad_query_gain, grad_key_gain]),
        ("dp", "tensor"),
    )
    return (
        both[0],
        both[1],
        gains[:model_width],
        summed[0],
        summed[1],
        summed[2],
        gains[2 * model_width : 2 * model_width + head_dim],
        gains[2 * model_width + head_dim :],
        grad_out_sum,
        gains[model_width : 2 * model_width],
        grad_w_gate_up,
        grad_w_down,
    )


def solution(mesh):
    in_specs = (
        P("dp", None),
        P("dp", None),
        P(),
        P(None, "tensor"),
        P(None, "tensor"),
        P(None, "tensor"),
        P(),
        P(),
        P("tensor", None),
        P(),
        P("dp", None, None, "tensor"),
        P("dp", "tensor", None),
        P("dp", None),
        P("dp", None),
        P("dp", None),
    )
    out_specs = (
        P("dp", None),
        P("dp", None),
        P(),
        P(None, "tensor"),
        P(None, "tensor"),
        P(None, "tensor"),
        P(),
        P(),
        P("tensor", None),
        P(),
        P("dp", None, None, "tensor"),
        P("dp", "tensor", None),
    )
    return jax.shard_map(local, mesh=mesh, in_specs=in_specs, out_specs=out_specs, check_vma=False)
```

profile of v0, /device:TPU:0, one launch (start us, length us, event | category | flops | bytes accessed | tf_op | source)
XLA Modules:
  0.0 1135.6 jit_solution(16545600781011678941)
XLA Ops:
  49.3 23.3 %reduce-scatter.6.cloned.1.call-done = bf16[128,2048]{1,0:T(8,128)(2,1)} async-done(((bf16[512,2048]{1,0:T(8,128)(2,1)}), bf16[128,2048]{1,0:T(8,128)(2,1)}) %reduce-scatter.6.cloned.1.call-update) | async-done | bytes 524304 | tf_op jit(solution)/shard_map/reduce_scatter | solution.py:156
  76.4 46.4 %all-gather.7.cloned.1.call-done = bf16[1024,2080]{1,0:T(8,128)(2,1)} async-done(((bf16[128,2080]{1,0:T(8,128)(2,1)}), bf16[1024,2080]{1,0:T(8,128)(2,1)}) %all-gather.7.cloned.1.call-update) | async-done | bytes 4259856 | tf_op jit(solution)/shard_map/all_gather | solution.py:108
  130.2 113.1 %all-gather.15.cloned.1.call-done = bf16[12,384,2048]{2,1,0:T(8,128)(2,1)} async-done(((bf16[3,384,2048]{2,1,0:T(8,128)(2,1)}), bf16[12,384,2048]{2,1,0:T(8,128)(2,1)}) %all-gather.15.cloned.1.call-update) | async-done | bytes 18874384 | tf_op jit(solution)/shard_map/all_gather | solution.py:125
  243.3 12.0 %fusion.12 = f32[1024,4,384]{2,0,1:T(8,128)} fusion(bf16[4,3,384,2048]{3,2,1,0:T(8,128)(2,1)} %bitcast.231, bf16[1024,2080]{1,0:T(8,128)(2,1)} %all-gather.7.cloned.1.call-done), kind=kOutput, calls=%fused_computation.30 | convolution fusion | flops 6442450944 | bytes 16777216 | tf_op jit(solution)/shard_map/td,rud->tru/dot_general | solution.py:167
  255.3 63.2 %all-gather.9.cloned.1.call-done = bf16[1024,2048]{1,0:T(8,128)(2,1)} async-done(((bf16[128,2048]{1,0:T(8,128)(2,1)}), bf16[1024,2048]{1,0:T(8,128)(2,1)}) %all-gather.9.cloned.1.call-update) | async-done | bytes 4194320 | tf_op jit(solution)/shard_map/all_gather | solution.py:164
  318.4 11.8 %fusion.9 = f32[1024,4,384]{2,0,1:T(8,128)} fusion(bf16[4,3,384,2048]{3,2,1,0:T(8,128)(2,1)} %bitcast.232, bf16[1024,2048]{1,0:T(8,128)(2,1)} %all-gather.9.cloned.1.call-done), kind=kOutput, calls=%fused_computation.27 | convolution fusion | flops 6442450944 | bytes 16777216 | tf_op jit(solution)/shard_map/td,rud->tru/dot_general | solution.py:167
  330.3 15.8 %multiply_convert_fusion.2 = (bf16[1024,4,384]{2,0,1:T(8,128)(2,1)}, bf16[1024,4,384]{2,0,1:T(8,128)(2,1)S(1)}, bf16[1024,4,384]{2,0,1:T(8,128)(2,1)}) fusion(f32[1024,4,384]{2,0,1:T(8,128)} %fusion.9, f32[1024,384]{1,0:T(8,128)S(1)} %copy-done.21, f32[1024,4,384]{2,0,1:T(8,128)} %fusion.12, bf16[4,3,384,2048]{3,2,1,0:T(8,128)(2,1)} %bitcast.233, ...), kind=kOutput, calls=%fused_computation.24 | convolution fusion | flops 6470762496 | bytes 34078720 | tf_op jit(solution)/shard_map/td,rud->tru/dot_general | solution.py:167
  346.0 10.0 fusion.8
  356.1 10.3 fusion.3
  366.5 86.9 %reduce-scatter.10.cloned.1.call-done = bf16[128,2048]{1,0:T(8,128)(2,1)} async-done(((bf16[1024,2048]{1,0:T(8,128)(2,1)}), bf16[128,2048]{1,0:T(8,128)(2,1)}) %reduce-scatter.10.cloned.1.call-update) | async-done | bytes 524304 | tf_op jit(solution)/shard_map/reduce_scatter | solution.py:187
  462.3 18.8 %all-gather.11.cloned.1.call-done = bf16[512,2048]{1,0:T(8,128)(2,1)} async-done(((bf16[128,2048]{1,0:T(8,128)(2,1)}), bf16[512,2048]{1,0:T(8,128)(2,1)}) %all-gather.11.cloned.1.call-update) | async-done | bytes 2097168 | tf_op jit(solution)/shard_map/all_gather | solution.py:210
  481.2 5.3 fusion.35
  516.1 11.0 bitcast_convert_fusion
  541.9 5.5 reduce-scatter.12.cloned.1.call-done
  548.8 90.9 %reduce-scatter.8.cloned.1.call-done = bf16[128,2048]{1,0:T(8,128)(2,1)} async-done(((bf16[1024,2048]{1,0:T(8,128)(2,1)}), bf16[128,2048]{1,0:T(8,128)(2,1)}) %reduce-scatter.8.cloned.1.call-update) | async-done | bytes 524304 | tf_op jit(solution)/shard_map/reduce_scatter | solution.py:177
  643.4 9.8 convert_bitcast_fusion
  653.2 7.4 convert_bitcast_fusion.1
  660.6 7.4 convert_bitcast_fusion.2
  670.2 6.7 copy.190
  677.6 43.3 %psum.35 = f32[4352]{0:T(1024)S(1)} all-reduce(f32[4352]{0:T(1024)S(1)} %pad_maximum_fusion.8), channel_id=1, replica_groups=mesh['dp'=8,'tensor'=4] {'dp','tensor'}, use_global_device_ids=true, to_apply=%region_23.24 | all-reduce | flops 4352 | bytes 34816 | tf_op jit(solution)/shard_map/psum | solution.py:268
  722.1 221.7 %all-reduce.3.cloned.1.call-done = (bf16[2048,1024]{1,0:T(8,128)(2,1)}, bf16[2048,128]{1,0:T(8,128)(2,1)}, bf16[2048,128]{1,0:T(8,128)(2,1)}, bf16[1024,2048]{1,0:T(8,128)(2,1)}) async-done(((bf16[2048,1024]{1,0:T(8,128)(2,1)}, bf16[2048,128]{1,0:T(8,128)(2,1)}, bf16[2048,128]{1,0:T(8,128)(2,1)}, bf16[1024,2048]{1,0:T(8,128)(2,1)}), (bf16[2048,1024]{1,0:T(8,128)(2,1)}, bf16[2048,128]{1,0:T(8,128)(2,1)}, ...) | async-done | bytes 9437200 | tf_op jit(solution)/shard_map/psum | solution.py:264
  943.8 6.8 convert_element_type.187
  957.1 22.2 %all-gather.13.cloned.1.call-done = bf16[2,512,2048]{2,1,0:T(8,128)(2,1)} async-done(((bf16[2,128,2048]{2,1,0:T(8,128)(2,1)}), bf16[2,512,2048]{2,1,0:T(8,128)(2,1)}) %all-gather.13.cloned.1.call-update) | async-done | bytes 4194320 | tf_op jit(solution)/shard_map/all_gather | solution.py:259
  984.1 135.6 %reduce-scatter.14.cloned.1.call-done = bf16[1152,2048]{1,0:T(8,128)(2,1)} async-done(((bf16[4608,2048]{1,0:T(8,128)(2,1)}), bf16[1152,2048]{1,0:T(8,128)(2,1)}) %reduce-scatter.14.cloned.1.call-update) | async-done | bytes 4718608 | tf_op jit(solution)/shard_map/reduce_scatter | solution.py:199
  (254 shorter events, 133.4 us)
Async XLA Ops:
  8.0 11.3 copy-start
  8.0 64.6 %reduce-scatter.6.cloned.1.call-start = ((), (), s32[]{:S(2)}) async-start(), calls=%async_computation.5 | async-start | bytes 2621440 | tf_op jit(solution)/shard_map/reduce_scatter | solution.py:156
  8.1 14.6 %copy-start.51 = (f32[64]{0:T(128)}, f32[64]{0:T(128)S(1)}, u32[]{:S(2)}) copy-start(f32[64]{0:T(128)S(1)} %multiply_exponential_fusion) | copy-start | bytes 772
  10.0 12.7 %copy-start.40 = (f32[512]{0:T(512)}, f32[512]{0:T(512)S(1)}, u32[]{:S(2)}) copy-start(f32[512]{0:T(512)S(1)} %subtract_convert_fusion.2) | copy-start | bytes 6148
  38.6 84.3 %all-gather.7.cloned.1.call-start = ((), (), s32[]{:S(2)}) async-start(), calls=%async_computation.6 | async-start | bytes 5013504 | tf_op jit(solution)/shard_map/all_gather | solution.py:108
  44.2 199.1 %all-gather.15.cloned.1.call-start = ((), (), s32[]{:S(2)}) async-start(), calls=%async_computation.14 | async-start | bytes 23592960 | tf_op jit(solution)/shard_map/all_gather | solution.py:125
  49.2 24.9 %copy-start.33 = (f32[2048]{0:T(1024)S(1)}, f32[2048]{0:T(1024)}, u32[]{:S(2)}) copy-start(f32[2048]{0:T(1024)} %param.24) | copy-start | bytes 24580
  49.3 269.2 %all-gather.9.cloned.1.call-start = ((), (), s32[]{:S(2)}) async-start(), calls=%async_computation.7 | async-start | bytes 4718592 | tf_op jit(solution)/shard_map/all_gather | solution.py:164
  74.1 50.1 %copy-start.44 = (f32[128]{0:T(128)}, f32[128]{0:T(128)S(1)}, u32[]{:S(2)}) copy-start(f32[128]{0:T(128)S(1)} %add_rsqrt_fusion.4) | copy-start | bytes 1540
  76.4 377.0 %reduce-scatter.10.cloned.1.call-start = ((), (), s32[]{:S(2)}) async-start(), calls=%async_computation.9 | async-start | bytes 4718592 | tf_op jit(solution)/shard_map/reduce_scatter | solution.py:187
  318.4 11.8 %copy-start.21 = (f32[1024,384]{1,0:T(8,128)S(1)}, f32[1024,384]{1,0:T(8,128)}, u32[]{:S(2)}) copy-start(f32[1024,384]{1,0:T(8,128)} %copy.173) | copy-start | bytes 4718596
  346.0 10.0 copy-start.65
  366.4 86.9 %copy-start.5 = (bf16[128,2048]{1,0:T(8,128)(2,1)S(1)}, bf16[128,2048]{1,0:T(8,128)(2,1)}, u32[]{:S(2)}) copy-start(bf16[128,2048]{1,0:T(8,128)(2,1)} %reduce-scatter.6.cloned.1.call-done) | copy-start | bytes 1572868
  366.4 114.8 %all-gather.11.cloned.1.call-start = ((), (), s32[]{:S(2)}) async-start(), calls=%async_computation.10 | async-start | bytes 2621440 | tf_op jit(solution)/shard_map/all_gather | solution.py:210
  458.9 88.5 %reduce-scatter.12.cloned.1.call-start = ((), (), s32[]{:S(2)}) async-start(), calls=%async_computation.11 | async-start | bytes 2621440 | tf_op jit(solution)/shard_map/reduce_scatter | solution.py:256
  481.2 10.4 slice-start
  516.0 123.7 %reduce-scatter.8.cloned.1.call-start = ((), (), s32[]{:S(2)}) async-start(), calls=%async_computation.8 | async-start | bytes 4718592 | tf_op jit(solution)/shard_map/reduce_scatter | solution.py:177
  527.1 416.6 %all-reduce.3.cloned.1.call-start = ((), (), s32[]{:S(2)}) async-start(), calls=%async_computation.15 | async-start | bytes 18874368 | tf_op jit(solution)/shard_map/psum | solution.py:264
  541.2 98.5 %copy-start.7 = (bf16[128,2048]{1,0:T(8,128)(2,1)S(1)}, bf16[128,2048]{1,0:T(8,128)(2,1)}, u32[]{:S(2)}) copy-start(bf16[128,2048]{1,0:T(8,128)(2,1)} %reduce-scatter.10.cloned.1.call-done) | copy-start | bytes 1572868
  541.2 98.5 %copy-start.34 = (f32[2048]{0:T(1024)S(1)}, f32[2048]{0:T(1024)}, u32[]{:S(2)}) copy-start(f32[2048]{0:T(1024)} %param.24) | copy-start | bytes 24580
  541.2 98.5 %copy-start.45 = (f32[128]{0:T(128)S(1)}, f32[128]{0:T(128)}, u32[]{:S(2)}) copy-start(f32[128]{0:T(128)} %copy-done.44) | copy-start | bytes 1540
  541.2 98.5 %copy-start.54 = (f32[128]{0:T(128)S(1)}, f32[128]{0:T(128)}, u32[]{:S(2)}) copy-start(f32[128]{0:T(128)} %copy-done.53) | copy-start | bytes 1540
  541.3 438.0 %all-gather.13.cloned.1.call-start = ((), (), s32[]{:S(2)}) async-start(), calls=%async_computation.12 | async-start | bytes 5242880 | tf_op jit(solution)/shard_map/all_gather | solution.py:259
  643.1 476.6 %reduce-scatter.14.cloned.1.call-start = ((), (), s32[]{:S(2)}) async-start(), calls=%async_computation.13 | async-start | bytes 23592960 | tf_op jit(solution)/shard_map/reduce_scatter | solution.py:199
  (58 other events, 214.4 us)
Sparse Core Ops, SparseCore 0:
  38.7 33.9 reduce-scatter.5
  459.0 22.1 all-gather.10
  516.1 31.1 reduce-scatter.11
  551.4 88.2 reduce-scatter.7
  645.2 298.5 all-reduce.2
  945.8 33.4 all-gather.12
  981.9 137.8 reduce-scatter.13
Sparse Core Ops, SparseCore 1:
  44.3 78.5 all-gather.6
  124.9 118.3 all-gather.14
  245.9 72.5 all-gather.8
  366.5 86.8 reduce-scatter.9
where the time goes:
time: 1140 us
  waiting for transfers between devices  828 us (73%)
  matrix products  146 us (13%)
  local copies, waits for them, and re-layouts  50.5 us (4%)
  other arithmetic  49.9 us (4%)
  blocking collectives  43.3 us (4%)
  between operations  17 us (1%)
    psum x1, waiting for transfers between devices, local(): lax.psum(grad_query_weight.astype(bf), 'dp').astype(f32)  222 us
    reduce_scatter x1, waiting for transfers between devices, local(): lax.psum_scatter(weight_grads.reshape(-1, model_width), 'tensor', tiled=T...  136 us
    all_gather x1, waiting for transfers between devices, local(): all_weights = lax.all_gather(own_weights, 'tensor')  113 us
    reduce_scatter x1, waiting for transfers between devices, local(): mixture = lax.psum_scatter(mixture_part, 'dp', tiled=True).astype(f32)  90.9 us
    reduce_scatter x1, waiting for transfers between devices, local(): lax.psum_scatter(grad_normed_part.astype(bf), 'dp', tiled=True).astype(f32)  86.9 us
    all_gather x1, waiting for transfers between devices, local(): inputs = lax.all_gather(normed_two, 'dp', tiled=True)  63.2 us
    all_gather x1, waiting for transfers between devices, local(): gathered = lax.all_gather(packed, 'dp', tiled=True)  46.4 us
    psum x1, blocking collectives, local(): lax.psum(jnp.concatenate([grad_gain_one, grad_gain_two, grad_query_gain,...  43.3 us
  transfers between devices with their start and end apart: 11, of which 11 were waited for; matrix products, arithmetic and copies ran while one was open for 10% of the time, Pallas kernels for 0%

commit v1 on v0

--- a/solution.py
+++ b/solution.py
@@ -6,6 +6,28 @@
 
 EPSILON = 1e-06
 ROPE_BASE = 1000000.0
+
+
+def joined_along(parts, dim):
+    parts = jnp.moveaxis(parts, 0, dim)
+    shape = parts.shape
+    return parts.reshape(*shape[:dim], shape[dim] * shape[dim + 1], *shape[dim + 2 :])
+
+
+def collect(value, axis, dim):
+    size = lax.axis_size(axis)
+    pairs = [(i, (i + 1) % size) for i in range(size)]
+    back = [(b, a) for a, b in pairs]
+    lower, upper = ([], [])
+    for hop in range(size - 1):
+        if hop % 2 == 0:
+            lower.append(lax.ppermute(lower[-1] if lower else value, axis, pairs))
+        else:
+            upper.append(lax.ppermute(upper[-1] if upper else value, axis, back))
+    blocks = jnp.stack([*lower[::-1], value, *upper])
+    shift = lax.axis_index(axis) - len(lower)
+    blocks = blocks[(jnp.arange(size) - shift) % size]
+    return joined_along(blocks, dim)
 
 
 def rms_parts(values):
@@ -161,7 +183,7 @@
     middle = hidden_q + attention
     hat_two, inv_two = rms_parts(middle)
     normed_two = (hat_two * norm2_gain).astype(bf)
-    inputs = lax.all_gather(normed_two, "dp", tiled=True)
+    inputs = collect(normed_two, "dp", 0)
 
     def project(left, which):
         return jnp.einsum("td,rud->tru", left, all_weights[:, which], preferred_element_type=f32)

time: 1140 us -> 1130 us (level)
  waiting for transfers between devices: 828 us -> 779 us
  local copies, waits for them, and re-layouts: 50.5 us -> 69 us
  starting transfers between devices: 0.85 us -> 19.1 us
    ppermute x0 -> x7, waiting for transfers between devices: none -> 89.3 us  [the longest x4 89.3 us: collect(): lower.append(lax.ppermute(lower[-1] if lower else value, axis, pairs))]
    all_gather x1 -> x0, waiting for transfers between devices: 63.2 us -> none  [local(): inputs = lax.all_gather(normed_two, 'dp', tiled=True)]
    all_gather x1, waiting for transfers between devices: 46.4 us -> 0.01 us  [local(): gathered = lax.all_gather(packed, 'dp', tiled=True)]
    all_gather x1, waiting for transfers between devices: 113 us -> 82.7 us  [local(): all_weights = lax.all_gather(own_weights, 'tensor')]
    ppermute x0 -> x7, starting transfers between devices: none -> 18.3 us  [the longest x3 14.1 us: collect(): upper.append(lax.ppermute(upper[-1] if upper else value, axis, back))]
    unnamed x146 -> x157, local copies, waits for them, and re-layouts: 14.4 us -> 26.9 us
  transfers between devices with their start and end apart: 11 -> 17, of which waited for: 11 -> 13; matrix products, arithmetic and copies ran while one was open for 10% -> 11% of each run, Pallas kernels for 0% -> 0%
where the time goes in v1:
time: 1130 us; the launch traced here: 1120 us
  waiting for transfers between devices  779 us (69%)
  matrix products  147 us (13%)
  local copies, waits for them, and re-layouts  69 us (6%)
  other arithmetic  49.7 us (4%)
  blocking collectives  43.1 us (4%)
  starting transfers between devices  19.1 us (2%)
  between operations  17 us (2%)
    psum x1, waiting for transfers between devices, local(): lax.psum(grad_query_weight.astype(bf), 'dp').astype(f32)  222 us
    reduce_scatter x1, waiting for transfers between devices, local(): lax.psum_scatter(weight_grads.reshape(-1, model_width), 'tensor', tiled=T...  136 us
    reduce_scatter x1, waiting for transfers between devices, local(): mixture = lax.psum_scatter(mixture_part, 'dp', tiled=True).astype(f32)  91 us
    ppermute x4, waiting for transfers between devices, collect(): lower.append(lax.ppermute(lower[-1] if lower else value, axis, pairs))  89.3 us
    reduce_scatter x1, waiting for transfers between devices, local(): lax.psum_scatter(grad_normed_part.astype(bf), 'dp', tiled=True).astype(f32)  88.3 us
    all_gather x1, waiting for transfers between devices, local(): all_weights = lax.all_gather(own_weights, 'tensor')  82.7 us
    psum x1, blocking collectives, local(): lax.psum(jnp.concatenate([grad_gain_one, grad_gain_two, grad_query_gain,...  43.1 us
    dot_general x3, matrix products, project(): jnp.einsum('td,rud->tru', left, all_weights[:, which], preferred_element_...  39.9 us
  transfers between devices with their start and end apart: 17, of which 13 were waited for; matrix products, arithmetic and copies ran while one was open for 11% of the time, Pallas kernels for 0%

profile of v1, /device:TPU:0, one launch (start us, length us, event | category | flops | bytes accessed | tf_op | source)
XLA Modules:
  0.0 1123.1 jit_solution(1281838814658535848)
XLA Ops:
  49.3 23.3 %reduce-scatter.6.cloned.1.call-done = bf16[128,2048]{1,0:T(8,128)(2,1)} async-done(((bf16[512,2048]{1,0:T(8,128)(2,1)}), bf16[128,2048]{1,0:T(8,128)(2,1)}) %reduce-scatter.6.cloned.1.call-update) | async-done | bytes 524304 | tf_op jit(solution)/shard_map/reduce_scatter | solution.py:178
  77.1 21.4 %collective-permute-done = bf16[128,2048]{1,0:T(8,128)(2,1)S(1)} collective-permute-done((bf16[128,2048]{1,0:T(8,128)(2,1)S(1)}, bf16[128,2048]{1,0:T(8,128)(2,1)S(1)}, u32[]{:S(2)}, u32[]{:S(2)}) %collective-permute-start) | collective-permute-done | bytes 524320 | tf_op jit(solution)/shard_map/ppermute | solution.py:24
  103.1 29.2 %collective-permute-done.1 = bf16[128,2048]{1,0:T(8,128)(2,1)S(1)} collective-permute-done((bf16[128,2048]{1,0:T(8,128)(2,1)S(1)}, bf16[128,2048]{1,0:T(8,128)(2,1)S(1)}, u32[]{:S(2)}, u32[]{:S(2)}) %collective-permute-start.1) | collective-permute-done | bytes 524320 | tf_op jit(solution)/shard_map/ppermute | solution.py:24
  139.7 22.3 %collective-permute-done.2 = bf16[128,2048]{1,0:T(8,128)(2,1)} collective-permute-done((bf16[128,2048]{1,0:T(8,128)(2,1)S(1)}, bf16[128,2048]{1,0:T(8,128)(2,1)}, u32[]{:S(2)}, u32[]{:S(2)}) %collective-permute-start.2) | collective-permute-done | bytes 524320 | tf_op jit(solution)/shard_map/ppermute | solution.py:24
  167.3 16.5 %collective-permute-done.3 = bf16[128,2048]{1,0:T(8,128)(2,1)} collective-permute-done((bf16[128,2048]{1,0:T(8,128)(2,1)}, bf16[128,2048]{1,0:T(8,128)(2,1)}, u32[]{:S(2)}, u32[]{:S(2)}) %collective-permute-start.3) | collective-permute-done | bytes 524320 | tf_op jit(solution)/shard_map/ppermute | solution.py:24
  209.5 82.7 %all-gather.12.cloned.1.call-done = bf16[12,384,2048]{2,1,0:T(8,128)(2,1)} async-done(((bf16[3,384,2048]{2,1,0:T(8,128)(2,1)}), bf16[12,384,2048]{2,1,0:T(8,128)(2,1)}) %all-gather.12.cloned.1.call-update) | async-done | bytes 18874384 | tf_op jit(solution)/shard_map/all_gather | solution.py:147
  292.3 11.9 %fusion.9 = f32[1024,4,384]{2,0,1:T(8,128)} fusion(bf16[1024,2048,1]{1,0,2:T(8,128)(2,1)} %bitcast.240, bf16[4,3,384,2048]{3,2,1,0:T(8,128)(2,1)} %bitcast.251), kind=kOutput, calls=%fused_computation.28 | convolution fusion | flops 6442450944 | bytes 16777216 | tf_op jit(solution)/shard_map/td,rud->tru/dot_general | solution.py:189
  304.1 11.9 %fusion.12 = f32[1024,4,384]{2,0,1:T(8,128)} fusion(bf16[4,3,384,2048]{3,2,1,0:T(8,128)(2,1)} %bitcast.252, bf16[1024,2080]{1,0:T(8,128)(2,1)} %all-gather.6.cloned.1.call-done), kind=kOutput, calls=%fused_computation.31 | convolution fusion | flops 6442450944 | bytes 16777216 | tf_op jit(solution)/shard_map/td,rud->tru/dot_general | solution.py:189
  316.0 16.2 %multiply_convert_fusion.2 = (bf16[1024,4,384]{2,0,1:T(8,128)(2,1)}, bf16[1024,4,384]{2,0,1:T(8,128)(2,1)}, bf16[1024,4,384]{2,0,1:T(8,128)(2,1)}) fusion(f32[1024,4,384]{2,0,1:T(8,128)} %fusion.9, f32[1024,384]{1,0:T(8,128)} %copy.173, f32[1024,4,384]{2,0,1:T(8,128)} %fusion.12, bf16[1024,2048,1]{1,0,2:T(8,128)(2,1)S(1)} %bitcast.242, ...), kind=kOutput, calls=%fused_computation.25 | convolution fusion | flops 6470762496 | bytes 34078720 | tf_op jit(solution)/shard_map/td,rud->tru/dot_general | solution.py:189
  332.2 9.9 fusion.8
  342.0 10.3 fusion.3
  352.4 88.3 %reduce-scatter.10.cloned.1.call-done = bf16[128,2048]{1,0:T(8,128)(2,1)} async-done(((bf16[1024,2048]{1,0:T(8,128)(2,1)}), bf16[128,2048]{1,0:T(8,128)(2,1)}) %reduce-scatter.10.cloned.1.call-update) | async-done | bytes 524304 | tf_op jit(solution)/shard_map/reduce_scatter | solution.py:209
  449.7 18.9 %all-gather.8.cloned.1.call-done = bf16[512,2048]{1,0:T(8,128)(2,1)} async-done(((bf16[128,2048]{1,0:T(8,128)(2,1)}), bf16[512,2048]{1,0:T(8,128)(2,1)}) %all-gather.8.cloned.1.call-update) | async-done | bytes 2097168 | tf_op jit(solution)/shard_map/all_gather | solution.py:232
  503.5 11.0 bitcast_convert_fusion
  536.3 91.0 %reduce-scatter.8.cloned.1.call-done = bf16[128,2048]{1,0:T(8,128)(2,1)} async-done(((bf16[1024,2048]{1,0:T(8,128)(2,1)}), bf16[128,2048]{1,0:T(8,128)(2,1)}) %reduce-scatter.8.cloned.1.call-update) | async-done | bytes 524304 | tf_op jit(solution)/shard_map/reduce_scatter | solution.py:199
  630.8 10.0 convert_bitcast_fusion.1
  640.9 7.4 convert_bitcast_fusion.2
  648.3 7.3 convert_bitcast_fusion
  657.9 6.7 copy.190
  665.3 43.1 %psum.35 = f32[4352]{0:T(1024)S(1)} all-reduce(f32[4352]{0:T(1024)S(1)} %pad_maximum_fusion.8), channel_id=1, replica_groups=mesh['dp'=8,'tensor'=4] {'dp','tensor'}, use_global_device_ids=true, to_apply=%region_23.24 | all-reduce | flops 4352 | bytes 34816 | tf_op jit(solution)/shard_map/psum | solution.py:290
  709.5 221.8 %all-reduce.3.cloned.1.call-done = (bf16[2048,1024]{1,0:T(8,128)(2,1)}, bf16[2048,128]{1,0:T(8,128)(2,1)}, bf16[2048,128]{1,0:T(8,128)(2,1)}, bf16[1024,2048]{1,0:T(8,128)(2,1)}) async-done(((bf16[2048,1024]{1,0:T(8,128)(2,1)}, bf16[2048,128]{1,0:T(8,128)(2,1)}, bf16[2048,128]{1,0:T(8,128)(2,1)}, bf16[1024,2048]{1,0:T(8,128)(2,1)}), (bf16[2048,1024]{1,0:T(8,128)(2,1)}, bf16[2048,128]{1,0:T(8,128)(2,1)}, ...) | async-done | bytes 9437200 | tf_op jit(solution)/shard_map/psum | solution.py:286
  931.3 6.8 convert_element_type.187
  944.6 22.2 %all-gather.10.cloned.1.call-done = bf16[2,512,2048]{2,1,0:T(8,128)(2,1)} async-done(((bf16[2,128,2048]{2,1,0:T(8,128)(2,1)}), bf16[2,512,2048]{2,1,0:T(8,128)(2,1)}) %all-gather.10.cloned.1.call-update) | async-done | bytes 4194320 | tf_op jit(solution)/shard_map/all_gather | solution.py:281
  971.6 135.6 %reduce-scatter.14.cloned.1.call-done = bf16[1152,2048]{1,0:T(8,128)(2,1)} async-done(((bf16[4608,2048]{1,0:T(8,128)(2,1)}), bf16[1152,2048]{1,0:T(8,128)(2,1)}) %reduce-scatter.14.cloned.1.call-update) | async-done | bytes 4718608 | tf_op jit(solution)/shard_map/reduce_scatter | solution.py:221
  (281 shorter events, 180.7 us)
Async XLA Ops:
  8.0 64.6 %reduce-scatter.6.cloned.1.call-start = ((), (), s32[]{:S(2)}) async-start(), calls=%async_computation.5 | async-start | bytes 2621440 | tf_op jit(solution)/shard_map/reduce_scatter | solution.py:178
  38.6 163.7 %all-gather.6.cloned.1.call-start = ((), (), s32[]{:S(2)}) async-start(), calls=%async_computation.6 | async-start | bytes 5013504 | tf_op jit(solution)/shard_map/all_gather | solution.py:130
  44.2 248.0 %all-gather.12.cloned.1.call-start = ((), (), s32[]{:S(2)}) async-start(), calls=%async_computation.13 | async-start | bytes 23592960 | tf_op jit(solution)/shard_map/all_gather | solution.py:147
  49.3 391.4 %reduce-scatter.10.cloned.1.call-start = ((), (), s32[]{:S(2)}) async-start(), calls=%async_computation.8 | async-start | bytes 4718592 | tf_op jit(solution)/shard_map/reduce_scatter | solution.py:209
  74.1 87.9 %copy-start.46 = (f32[128]{0:T(128)}, f32[128]{0:T(128)S(1)}, u32[]{:S(2)}) copy-start(f32[128]{0:T(128)S(1)} %add_rsqrt_fusion.4) | copy-start | bytes 1540
  75.5 22.9 %collective-permute-start = (bf16[128,2048]{1,0:T(8,128)(2,1)S(1)}, bf16[128,2048]{1,0:T(8,128)(2,1)S(1)}, u32[]{:S(2)}, u32[]{:S(2)}) collective-permute-start(bf16[128,2048]{1,0:T(8,128)(2,1)S(1)} %multiply_convert_fusion.3), channel_id=1, source_target_pairs={{0,4},{4,8},{8,12},{12,16},{16,20},{20,24},{24,28},{28,0},{1,5},{5... | collective-permute-start | bytes 1572872 | tf_op jit(solution)/shard_map/ppermute | solution.py:24
  98.4 36.4 %copy-start.29 = (bf16[128,2048]{1,0:T(8,128)(2,1)}, bf16[128,2048]{1,0:T(8,128)(2,1)S(1)}, u32[]{:S(2)}) copy-start(bf16[128,2048]{1,0:T(8,128)(2,1)S(1)} %collective-permute-done) | copy-start | bytes 1572868
  98.4 33.9 %collective-permute-start.1 = (bf16[128,2048]{1,0:T(8,128)(2,1)S(1)}, bf16[128,2048]{1,0:T(8,128)(2,1)S(1)}, u32[]{:S(2)}, u32[]{:S(2)}) collective-permute-start(bf16[128,2048]{1,0:T(8,128)(2,1)S(1)} %collective-permute-done), channel_id=1, source_target_pairs={{0,4},{4,8},{8,12},{12,16},{16,20},{20,24},{24,28},{28,0},{1,5},{5... | collective-permute-start | bytes 1572872 | tf_op jit(solution)/shard_map/ppermute | solution.py:24
  98.6 36.2 %collective-permute-start.4 = (bf16[128,2048]{1,0:T(8,128)(2,1)S(1)}, bf16[128,2048]{1,0:T(8,128)(2,1)}, u32[]{:S(2)}, u32[]{:S(2)}) collective-permute-start(bf16[128,2048]{1,0:T(8,128)(2,1)S(1)} %multiply_convert_fusion.3), channel_id=1, source_target_pairs={{4,0},{8,4},{12,8},{16,12},{20,16},{24,20},{28,24},{0,28},{5,1},{9... | collective-permute-start | bytes 1572872 | tf_op jit(solution)/shard_map/ppermute | solution.py:26
  132.3 29.6 %collective-permute-start.2 = (bf16[128,2048]{1,0:T(8,128)(2,1)S(1)}, bf16[128,2048]{1,0:T(8,128)(2,1)}, u32[]{:S(2)}, u32[]{:S(2)}) collective-permute-start(bf16[128,2048]{1,0:T(8,128)(2,1)S(1)} %collective-permute-done.1), channel_id=1, source_target_pairs={{0,4},{4,8},{8,12},{12,16},{16,20},{20,24},{24,28},{28,0},{1,5},{5... | collective-permute-start | bytes 1572872 | tf_op jit(solution)/shard_map/ppermute | solution.py:24
  134.8 27.8 %collective-permute-start.5 = (bf16[128,2048]{1,0:T(8,128)(2,1)}, bf16[128,2048]{1,0:T(8,128)(2,1)}, u32[]{:S(2)}, u32[]{:S(2)}) collective-permute-start(bf16[128,2048]{1,0:T(8,128)(2,1)} %collective-permute-done.4), channel_id=1, source_target_pairs={{4,0},{8,4},{12,8},{16,12},{20,16},{24,20},{28,24},{0,28},{5,1},{9... | collective-permute-start | bytes 1572872 | tf_op jit(solution)/shard_map/ppermute | solution.py:26
  162.0 21.8 %collective-permute-start.3 = (bf16[128,2048]{1,0:T(8,128)(2,1)}, bf16[128,2048]{1,0:T(8,128)(2,1)}, u32[]{:S(2)}, u32[]{:S(2)}) collective-permute-start(bf16[128,2048]{1,0:T(8,128)(2,1)} %collective-permute-done.2), channel_id=1, source_target_pairs={{0,4},{4,8},{8,12},{12,16},{16,20},{20,24},{24,28},{28,0},{1,5},{5... | collective-permute-start | bytes 1572872 | tf_op jit(solution)/shard_map/ppermute | solution.py:24
  162.6 33.6 %collective-permute-start.6 = (bf16[128,2048]{1,0:T(8,128)(2,1)}, bf16[128,2048]{1,0:T(8,128)(2,1)S(1)}, u32[]{:S(2)}, u32[]{:S(2)}) collective-permute-start(bf16[128,2048]{1,0:T(8,128)(2,1)} %collective-permute-done.5), channel_id=1, source_target_pairs={{4,0},{8,4},{12,8},{16,12},{20,16},{24,20},{28,24},{0,28},{5,1},{9... | collective-permute-start | bytes 1572872 | tf_op jit(solution)/shard_map/ppermute | solution.py:26
  352.3 88.3 %copy-start.5 = (bf16[128,2048]{1,0:T(8,128)(2,1)S(1)}, bf16[128,2048]{1,0:T(8,128)(2,1)}, u32[]{:S(2)}) copy-start(bf16[128,2048]{1,0:T(8,128)(2,1)} %reduce-scatter.6.cloned.1.call-done) | copy-start | bytes 1572868
  352.4 116.2 %all-gather.8.cloned.1.call-start = ((), (), s32[]{:S(2)}) async-start(), calls=%async_computation.9 | async-start | bytes 2621440 | tf_op jit(solution)/shard_map/all_gather | solution.py:232
  446.3 88.5 %reduce-scatter.12.cloned.1.call-start = ((), (), s32[]{:S(2)}) async-start(), calls=%async_computation.10 | async-start | bytes 2621440 | tf_op jit(solution)/shard_map/reduce_scatter | solution.py:278
  503.5 123.8 %reduce-scatter.8.cloned.1.call-start = ((), (), s32[]{:S(2)}) async-start(), calls=%async_computation.7 | async-start | bytes 4718592 | tf_op jit(solution)/shard_map/reduce_scatter | solution.py:199
  514.6 416.7 %all-reduce.3.cloned.1.call-start = ((), (), s32[]{:S(2)}) async-start(), calls=%async_computation.14 | async-start | bytes 18874368 | tf_op jit(solution)/shard_map/psum | solution.py:286
  528.7 98.6 %copy-start.7 = (bf16[128,2048]{1,0:T(8,128)(2,1)S(1)}, bf16[128,2048]{1,0:T(8,128)(2,1)}, u32[]{:S(2)}) copy-start(bf16[128,2048]{1,0:T(8,128)(2,1)} %reduce-scatter.10.cloned.1.call-done) | copy-start | bytes 1572868
  528.7 98.6 %copy-start.36 = (f32[2048]{0:T(1024)S(1)}, f32[2048]{0:T(1024)}, u32[]{:S(2)}) copy-start(f32[2048]{0:T(1024)} %param.24) | copy-start | bytes 24580
  528.7 98.6 %copy-start.47 = (f32[128]{0:T(128)S(1)}, f32[128]{0:T(128)}, u32[]{:S(2)}) copy-start(f32[128]{0:T(128)} %copy-done.46) | copy-start | bytes 1540
  528.7 98.6 %copy-start.56 = (f32[128]{0:T(128)S(1)}, f32[128]{0:T(128)}, u32[]{:S(2)}) copy-start(f32[128]{0:T(128)} %copy-done.55) | copy-start | bytes 1540
  528.7 438.0 %all-gather.10.cloned.1.call-start = ((), (), s32[]{:S(2)}) async-start(), calls=%async_computation.11 | async-start | bytes 5242880 | tf_op jit(solution)/shard_map/all_gather | solution.py:281
  630.6 476.6 %reduce-scatter.14.cloned.1.call-start = ((), (), s32[]{:S(2)}) async-start(), calls=%async_computation.12 | async-start | bytes 23592960 | tf_op jit(solution)/shard_map/reduce_scatter | solution.py:221
  (66 other events, 307.8 us)
Sparse Core Ops, SparseCore 0:
  38.7 33.9 reduce-scatter.5
  446.4 22.1 all-gather.7
  503.6 31.1 reduce-scatter.11
  538.8 88.3 reduce-scatter.7
  632.7 298.5 all-reduce.2
  933.2 33.4 all-gather.9
  969.3 137.8 reduce-scatter.13
Sparse Core Ops, SparseCore 1:
  44.3 117.9 all-gather.5
  164.3 127.9 all-gather.11
  352.5 88.2 reduce-scatter.9
